TPU v7x, 32 devices: a whole 2x2x4 slice. The times are simulated.
32 devices in a mesh: rows: 16 (over z, y, x), feat: 2 (over core).
Axes of the slice: x: 2, y: 2, z: 4, core: 2. Of those that a mesh axis runs over, the one named last changes fastest.
Arguments:
- queries: bfloat16 [1024, 128], P('rows', 'feat'), may hold values from -6 to 6
- corpus: bfloat16 [524288, 128], P(('rows', 'feat')), as said below
- candidates: int32 [1024, 100], P(('rows', 'feat')), may hold values from 0 to 524287, as said below
- threshold: int32 [1024], replicated, may hold values from 100 to 199, as said below
Outputs:
- exceed: float32 [1024], P(('rows', 'feat'))
- candidate_scores: float32 [1024, 100], P(('rows', 'feat'))
Inputs may be any that keep to these rules, and one draw needn't show every extreme that they name: Passage ids. Of the 3200 candidates of one device's queries (aligned blocks of 32 rows), at most 100 lie in the 16384 passages of any one device, and exactly 100 in some device's. `corpus`: passage embeddings of order one or smaller; their scale differs between passages. Some query has threshold 100 and some 199.
All inputs are finite; a program needn't handle non-finite values.
Results may differ from a plain program's by a relative error of at most 0.00035.
Values may be sent and summed in bfloat16 or wider, within the bound.
A program may use at most 64 MiB of HBM per device.

v0:
```python
import jax
import jax.numpy as jnp
from jax import lax
from jax.sharding import PartitionSpec as P


def body(queries, corpus, candidates, threshold):
    rows_dev = corpus.shape[0]
    width = corpus.shape[1]
    shards = lax.axis_size("rows") * lax.axis_size("feat")
    owned_queries = candidates.shape[0]
    per_query = candidates.shape[1]
    npass_all = rows_dev * shards
    cutoff = threshold.astype(jnp.float32) * 0.01
    owner = lax.axis_index(("rows", "feat"))
    full_rows = lax.all_gather(queries, "feat", axis=1, tiled=True)
    whole = lax.all_gather(full_rows, "rows", axis=0, tiled=True)
    query_count = whole.shape[0]
    block = 2048
    corpus_blocks = corpus.reshape(rows_dev // block, block, width)

    def visit(total, block_rows):
        scores = lax.dot_general(
            whole, block_rows, (((1,), (1,)), ((), ())), preferred_element_type=jnp.float32
        )
        return (total + jnp.sum(jnp.maximum(scores - cutoff[:, None], 0.0), axis=1), None)

    total, _ = lax.scan(visit, jnp.zeros((query_count,), jnp.float32), corpus_blocks)
    flat_ids = candidates.reshape(-1)
    total_ids = flat_ids.shape[0]
    capacity = (total_ids + shards - 1) // shards
    target = flat_ids // rows_dev
    onehot = (target[:, None] == jnp.arange(shards, dtype=jnp.int32)[None, :]).astype(jnp.int32)
    before = jnp.cumsum(onehot, axis=0) - onehot
    rank = jnp.sum(before * onehot, axis=1)
    query_ids = owner * owned_queries + jnp.arange(total_ids, dtype=jnp.int32) // per_query
    fields = jnp.stack([flat_ids - target * rows_dev, query_ids], axis=1)
    send_both = jnp.zeros((shards, capacity, 2), jnp.int32).at[target, rank].set(fields)
    n_rows = lax.axis_size("rows")
    n_feat = lax.axis_size("feat")
    received = lax.all_to_all(
        lax.all_to_all(
            send_both.reshape(n_rows, n_feat, capacity * 2),
            "rows",
            split_axis=0,
            concat_axis=0,
            tiled=True,
        ),
        "feat",
        split_axis=1,
        concat_axis=1,
        tiled=True,
    )
    received = received.reshape(shards * capacity, 2)
    picked = corpus[received[:, 0]]
    asked = whole[received[:, 1]]
    values = jnp.einsum("kd,kd->k", picked, asked, preferred_element_type=jnp.float32).reshape(
        n_rows, n_feat, capacity
    )
    partials = total.reshape(n_rows, n_feat, owned_queries)
    answers, mass_parts = (
        lax.all_to_all(
            lax.all_to_all(values, "rows", split_axis=0, concat_axis=0, tiled=True),
            "feat",
            split_axis=1,
            concat_axis=1,
            tiled=True,
        ),
        lax.all_to_all(
            lax.all_to_all(partials, "rows", split_axis=0, concat_axis=0, tiled=True),
            "feat",
            split_axis=1,
            concat_axis=1,
            tiled=True,
        ),
    )
    exceed = jnp.sum(mass_parts, axis=(0, 1)) * (8.0 / npass_all)
    candidate_scores = answers.reshape(shards, capacity)[target, rank].reshape(
        owned_queries, per_query
    )
    return (exceed, candidate_scores)


def solution(mesh):
    return jax.shard_map(
        body,
        mesh=mesh,
        in_specs=(P("rows", "feat"), P(("rows", "feat"), None), P(("rows", "feat"), None), P()),
        out_specs=(P(("rows", "feat")), P(("rows", "feat"), None)),
        check_vma=False,
    )
```

profile of v0, /device:TPU:0, one launch (start us, length us, event | category | flops | bytes accessed | tf_op | source)
XLA Modules:
  0.0 177.3 jit_solution(1144586767254924828)
XLA Ops:
  0.6 0.8 copy.40
  1.4 2.0 %all_gather.6 = bf16[64,128]{0,1:T(8,128)(2,1)S(1)} all-gather(bf16[64,64]{0,1:T(8,128)(2,1)S(1)} %copy.40), channel_id=1, replica_groups=mesh['rows'=16,'feat'=2] {'feat'}, dimensions={1}, use_global_device_ids=true | all-gather | bytes 24576 | tf_op jit(solution)/shard_map/all_gather | solution.py:16
  3.5 43.7 %all_gather.7 = bf16[1024,128]{1,0:T(8,128)(2,1)S(1)} all-gather(bf16[64,128]{1,0:T(8,128)(2,1)S(1)} %copy.41), channel_id=1, replica_groups=mesh['rows'=16,'feat'=2] {'rows'}, dimensions={0}, use_global_device_ids=true | all-gather | bytes 278528 | tf_op jit(solution)/shard_map/all_gather | solution.py:17
  47.9 18.8 %while.11 = (s32[]{:T(128)}, f32[1024]{0:T(1024)S(1)}, bf16[8,2048,128]{2,1,0:T(8,128)(2,1)}, bf16[1024,128]{1,0:T(8,128)(2,1)S(1)}, f32[1024]{0:T(1024)S(1)}, /*index=5*/s32[]{:T(128)}, s32[]{:T(128)}) while((s32[]{:T(128)}, f32[1024]{0:T(1024)S(1)}, bf16[8,2048,128]{2,1,0:T(8,128)(2,1)}, bf16[1024,128]{1,0:T(8,128)(2,1)S(1)}, ...), condition=%wide.region_2.3_spmd.clone, body=%wide.region_0.2_spmd.clone.sunk | while | flops 543163392 | bytes 807511 | solution.py:28
  47.9 2.3 %maximum_reduce_fusion.2 = f32[1024]{0:T(1024)S(1)} fusion(bf16[1024,128]{1,0:T(8,128)(2,1)S(1)} %get-tuple-element.115, f32[1024]{0:T(1024)S(1)} %get-tuple-element.116, bf16[8,2048,128]{2,1,0:T(8,128)(2,1)} %get-tuple-element.114, s32[]{:T(128)} %get-tuple-element.105), kind=kOutput, calls=%fused_computation.4.clone.1 | convolution fusion | flops 543161344 | bytes 795136 | tf_op jit(solution)/shard_map/while/body/eval_jaxpr/dot_general | solution.py:23
  50.2 2.3 %maximum_reduce_fusion.2 = f32[1024]{0:T(1024)S(1)} fusion(bf16[1024,128]{1,0:T(8,128)(2,1)S(1)} %get-tuple-element.115, f32[1024]{0:T(1024)S(1)} %get-tuple-element.116, bf16[8,2048,128]{2,1,0:T(8,128)(2,1)} %get-tuple-element.114, s32[]{:T(128)} %get-tuple-element.105), kind=kOutput, calls=%fused_computation.4.clone.1 | convolution fusion | flops 543161344 | bytes 795136 | tf_op jit(solution)/shard_map/while/body/eval_jaxpr/dot_general | solution.py:23
  52.6 2.3 %maximum_reduce_fusion.2 = f32[1024]{0:T(1024)S(1)} fusion(bf16[1024,128]{1,0:T(8,128)(2,1)S(1)} %get-tuple-element.115, f32[1024]{0:T(1024)S(1)} %get-tuple-element.116, bf16[8,2048,128]{2,1,0:T(8,128)(2,1)} %get-tuple-element.114, s32[]{:T(128)} %get-tuple-element.105), kind=kOutput, calls=%fused_computation.4.clone.1 | convolution fusion | flops 543161344 | bytes 795136 | tf_op jit(solution)/shard_map/while/body/eval_jaxpr/dot_general | solution.py:23
  54.9 2.3 %maximum_reduce_fusion.2 = f32[1024]{0:T(1024)S(1)} fusion(bf16[1024,128]{1,0:T(8,128)(2,1)S(1)} %get-tuple-element.115, f32[1024]{0:T(1024)S(1)} %get-tuple-element.116, bf16[8,2048,128]{2,1,0:T(8,128)(2,1)} %get-tuple-element.114, s32[]{:T(128)} %get-tuple-element.105), kind=kOutput, calls=%fused_computation.4.clone.1 | convolution fusion | flops 543161344 | bytes 795136 | tf_op jit(solution)/shard_map/while/body/eval_jaxpr/dot_general | solution.py:23
  57.3 2.3 %maximum_reduce_fusion.2 = f32[1024]{0:T(1024)S(1)} fusion(bf16[1024,128]{1,0:T(8,128)(2,1)S(1)} %get-tuple-element.115, f32[1024]{0:T(1024)S(1)} %get-tuple-element.116, bf16[8,2048,128]{2,1,0:T(8,128)(2,1)} %get-tuple-element.114, s32[]{:T(128)} %get-tuple-element.105), kind=kOutput, calls=%fused_computation.4.clone.1 | convolution fusion | flops 543161344 | bytes 795136 | tf_op jit(solution)/shard_map/while/body/eval_jaxpr/dot_general | solution.py:23
  59.6 2.3 %maximum_reduce_fusion.2 = f32[1024]{0:T(1024)S(1)} fusion(bf16[1024,128]{1,0:T(8,128)(2,1)S(1)} %get-tuple-element.115, f32[1024]{0:T(1024)S(1)} %get-tuple-element.116, bf16[8,2048,128]{2,1,0:T(8,128)(2,1)} %get-tuple-element.114, s32[]{:T(128)} %get-tuple-element.105), kind=kOutput, calls=%fused_computation.4.clone.1 | convolution fusion | flops 543161344 | bytes 795136 | tf_op jit(solution)/shard_map/while/body/eval_jaxpr/dot_general | solution.py:23
  62.0 2.3 %maximum_reduce_fusion.2 = f32[1024]{0:T(1024)S(1)} fusion(bf16[1024,128]{1,0:T(8,128)(2,1)S(1)} %get-tuple-element.115, f32[1024]{0:T(1024)S(1)} %get-tuple-element.116, bf16[8,2048,128]{2,1,0:T(8,128)(2,1)} %get-tuple-element.114, s32[]{:T(128)} %get-tuple-element.105), kind=kOutput, calls=%fused_computation.4.clone.1 | convolution fusion | flops 543161344 | bytes 795136 | tf_op jit(solution)/shard_map/while/body/eval_jaxpr/dot_general | solution.py:23
  64.3 2.3 %maximum_reduce_fusion.2 = f32[1024]{0:T(1024)S(1)} fusion(bf16[1024,128]{1,0:T(8,128)(2,1)S(1)} %get-tuple-element.115, f32[1024]{0:T(1024)S(1)} %get-tuple-element.116, bf16[8,2048,128]{2,1,0:T(8,128)(2,1)} %get-tuple-element.114, s32[]{:T(128)} %get-tuple-element.105), kind=kOutput, calls=%fused_computation.4.clone.1 | convolution fusion | flops 543161344 | bytes 795136 | tf_op jit(solution)/shard_map/while/body/eval_jaxpr/dot_general | solution.py:23
  67.3 4.1 %all-to-all-start = ((f32[16,2,32]{2,1,0:T(2,128)}), f32[16,2,32]{2,1,0:T(2,128)}, u32[]{:S(2)}, u32[]{:S(2)}) async-start(f32[16,2,32]{2,1,0:T(2,128)} %reshape.217), calls=%async_computation | async-start | bytes 32768 | tf_op jit(solution)/shard_map/all_to_all | solution.py:70
  71.9 9.2 %reduce-window.6 = s32[32,25,128]{2,1,0:T(8,128)S(1)} reduce-window(s32[32,25,128]{2,1,0:T(8,128)S(1)} %fusion.6, s32[]{:T(128)} %constant.28.clone.1), window={size=1x1x128 pad=0_0x0_0x127_0}, to_apply=%region_4.5 | reduce-window | flops 13004800 | bytes 819204 | tf_op jit(solution)/shard_map/reduce-window
  81.1 0.8 slice_reduce_fusion
  84.2 13.8 %scatter_custom_fusion = s32[3200,2]{1,0:T(8,128)S(1)} fusion(s32[3200]{0:T(1024)} %broadcast_select_fusion, s32[3200,2]{1,0:T(8,128)S(1)} %copy.44, s32[]{:T(128)} %constant.28.clone.1), kind=kCustom, calls=%fused_computation.11 | custom fusion | bytes 26112
  98.1 1.3 reshape.222
  99.4 0.7 copy.66
  100.2 3.7 %all_to_all.30 = f32[2,1,512]{2,1,0:T(1,128)S(1)} all-to-all(f32[2,1,512]{2,1,0:T(1,128)S(1)} %reshape.269), channel_id=1, replica_groups=mesh['rows'=16,'feat'=2] {'feat'}, dimensions={0} | all-to-all | bytes 8192 | tf_op jit(solution)/shard_map/all_to_all | solution.py:69
  103.8 6.8 %all-to-all-start.2 = ((s32[16,2,200]{2,1,0:T(2,128)}), s32[16,2,200]{2,1,0:T(2,128)S(1)}, u32[]{:S(2)}, u32[]{:S(2)}) async-start(s32[16,2,200]{2,1,0:T(2,128)} %reshape.222), calls=%async_computation.2 | async-start | bytes 65536 | tf_op jit(solution)/shard_map/all_to_all | solution.py:42
  112.5 5.6 %all-to-all-done.2 = s32[16,2,200]{2,1,0:T(2,128)S(1)} async-done(((s32[16,2,200]{2,1,0:T(2,128)}), s32[16,2,200]{2,1,0:T(2,128)S(1)}, u32[]{:S(2)}, u32[]{:S(2)}) %all-to-all-start.2) | async-done | bytes 25632 | tf_op jit(solution)/shard_map/all_to_all | solution.py:42
  118.1 3.7 %all_to_all.31 = s32[16,2,200]{2,0,1:T(8,128)S(1)} all-to-all(s32[16,2,200]{2,0,1:T(8,128)S(1)} %copy.45), channel_id=1, replica_groups=mesh['rows'=16,'feat'=2] {'feat'}, dimensions={1} | all-to-all | bytes 51200 | tf_op jit(solution)/shard_map/all_to_all | solution.py:41
  122.3 1.7 fusion.17
  124.0 1.9 %copy.57 = s32[3200,1]{0,1:T(1,128)S(1)} copy(s32[3200,1]{1,0:T(8,128)} %get-tuple-element.61) | data formatting | bytes 25600
  126.0 6.7 %gather_fusion.1 = bf16[3200,128]{1,0:T(8,128)(2,1)S(1)} fusion(bf16[1024,128]{1,0:T(8,128)(2,1)S(1)} %get-tuple-element.119, s32[4096]{0:T(1024)S(1)} %pad_clamp_fusion), kind=kCustom, calls=%fused_computation.1 | custom fusion | bytes 1651200 | tf_op jit(solution)/shard_map/gather | solution.py:56
  133.3 8.5 %gather_fusion = bf16[3200,128]{1,0:T(8,128)(2,1)S(1)} fusion(bf16[16384,128]{1,0:T(8,128)(2,1)} %bitcast.35, s32[4096]{0:T(1024)S(1)} %pad_clamp_fusion.1), kind=kCustom, calls=%fused_computation | custom fusion | bytes 1651200 | tf_op jit(solution)/shard_map/gather | solution.py:55
  142.4 0.7 reshape.224
  143.1 3.5 %all-to-all-start.4 = ((f32[16,2,100]{2,1,0:T(2,128)}), f32[16,2,100]{2,1,0:T(2,128)S(1)}, u32[]{:S(2)}, u32[]{:S(2)}) async-start(f32[16,2,100]{2,1,0:T(2,128)} %reshape.224), calls=%async_computation.4 | async-start | bytes 32768 | tf_op jit(solution)/shard_map/all_to_all | solution.py:63
  147.1 6.8 %all-to-all-done.4 = f32[16,2,100]{2,1,0:T(2,128)S(1)} async-done(((f32[16,2,100]{2,1,0:T(2,128)}), f32[16,2,100]{2,1,0:T(2,128)S(1)}, u32[]{:S(2)}, u32[]{:S(2)}) %all-to-all-start.4) | async-done | bytes 12832 | tf_op jit(solution)/shard_map/all_to_all | solution.py:63
  153.9 3.7 %all_to_all.32 = f32[16,2,100]{2,0,1:T(8,128)S(1)} all-to-all(f32[16,2,100]{2,0,1:T(8,128)S(1)} %copy.49), channel_id=1, replica_groups=mesh['rows'=16,'feat'=2] {'feat'}, dimensions={1} | all-to-all | bytes 25600 | tf_op jit(solution)/shard_map/all_to_all | solution.py:62
  157.6 19.0 %gather_fusion.2 = f32[3200]{0:T(1024)S(1)} fusion(f32[32,100]{1,0:T(8,128)S(1)} %bitcast.33, s32[3200]{0:T(1024)S(1)} %get-tuple-element.58), kind=kCustom, calls=%fused_computation.2 | custom fusion | bytes 51200 | tf_op jit(solution)/shard_map/gather | solution.py:78
  176.6 0.7 reshape.226
  (54 shorter events, 8.2 us)
Async XLA Ops:
  47.9 23.6 %copy-start = (s32[32,100]{1,0:T(8,128)S(1)}, s32[32,100]{1,0:T(8,128)}, u32[]{:S(2)}) copy-start(s32[32,100]{1,0:T(8,128)} %param.8) | copy-start | bytes 38404
  67.3 32.0 %all-to-all-start = ((f32[16,2,32]{2,1,0:T(2,128)}), f32[16,2,32]{2,1,0:T(2,128)}, u32[]{:S(2)}, u32[]{:S(2)}) async-start(f32[16,2,32]{2,1,0:T(2,128)} %reshape.217), calls=%async_computation | async-start | bytes 32768 | tf_op jit(solution)/shard_map/all_to_all | solution.py:70
  71.9 11.0 %copy-start.2 = (s32[2]{0:T(128)S(1)}, s32[2]{0:T(128)}, u32[]{:S(2)}) copy-start(s32[2]{0:T(128)} %constant.67) | copy-start | bytes 28
  71.9 11.1 %copy-start.1 = (s32[2]{0:T(128)S(1)}, s32[2]{0:T(128)}, u32[]{:S(2)}) copy-start(s32[2]{0:T(128)} %constant.64) | copy-start | bytes 28
  103.8 14.2 %all-to-all-start.2 = ((s32[16,2,200]{2,1,0:T(2,128)}), s32[16,2,200]{2,1,0:T(2,128)S(1)}, u32[]{:S(2)}, u32[]{:S(2)}) async-start(s32[16,2,200]{2,1,0:T(2,128)} %reshape.222), calls=%async_computation.2 | async-start | bytes 65536 | tf_op jit(solution)/shard_map/all_to_all | solution.py:42
  141.8 4.8 %copy-start.3 = (f32[32]{0:T(128)S(1)}, f32[32]{0:T(128)}, u32[]{:S(2)}) copy-start(f32[32]{0:T(128)} %bitcast_reduce_fusion) | copy-start | bytes 388
  143.1 10.8 %all-to-all-start.4 = ((f32[16,2,100]{2,1,0:T(2,128)}), f32[16,2,100]{2,1,0:T(2,128)S(1)}, u32[]{:S(2)}, u32[]{:S(2)}) async-start(f32[16,2,100]{2,1,0:T(2,128)} %reshape.224), calls=%async_computation.4 | async-start | bytes 32768 | tf_op jit(solution)/shard_map/all_to_all | solution.py:63
where the time goes:
time: 178 us; the launch traced here: 177 us
  local copies, waits for them, and re-layouts  59.9 us (34%)
  blocking collectives  56.8 us (32%)
  matrix products  18.5 us (10%)
  starting transfers between devices  14.4 us (8%)
  other arithmetic  14.1 us (8%)
  waiting for transfers between devices  12.4 us (7%)
    all_gather x1, blocking collectives, body(): whole = lax.all_gather(full_rows, 'rows', axis=0, tiled=True)  43.7 us
    gather x1, local copies, waits for them, and re-layouts, body(): answers.reshape(shards, capacity)[target, rank]  19 us
    dot_general x8, matrix products, visit(): lax.dot_general(whole, block_rows, (((1,), (1,)), ((), ())), preferred_el...  18.5 us
    unnamed x14, local copies, waits for them, and re-layouts  17.2 us
    another operation x3, other arithmetic  9.61 us
    gather x1, local copies, waits for them, and re-layouts, body(): picked = corpus[received[:, 0]]  8.49 us
    all_to_all x1, starting transfers between devices, body(): lax.all_to_all(send_both.reshape(n_rows, n_feat, capacity * 2), 'rows', s...  6.81 us
    all_to_all x1, waiting for transfers between devices, body(): lax.all_to_all(values, 'rows', split_axis=0, concat_axis=0, tiled=True)  6.78 us
  transfers between devices with their start and end apart: 3, of which 2 were waited for; matrix products, arithmetic and copies ran while one was open for 17% of the time, Pallas kernels for 0%

commit v1 on v0

--- a/solution.py
+++ b/solution.py
@@ -2,6 +2,24 @@
 import jax.numpy as jnp
 from jax import lax
 from jax.sharding import PartitionSpec as P
+
+
+def laid_out(blocks, dim):
+    blocks = jnp.moveaxis(blocks, 0, dim)
+    lengths = blocks.shape
+    return blocks.reshape(*lengths[:dim], lengths[dim] * lengths[dim + 1], *lengths[dim + 2 :])
+
+
+def doubled(value, axis):
+    peers = lax.axis_size(axis)
+    pieces = value[None]
+    for level in range(peers.bit_length() - 1):
+        bit = 1 << level
+        other = lax.ppermute(pieces, axis, [(i, i ^ bit) for i in range(peers)])
+        both = jnp.stack([pieces, other])
+        upper = lax.axis_index(axis) >> level & 1
+        pieces = jnp.where(upper == 0, both, both[::-1]).reshape(-1, *value.shape)
+    return pieces
 
 
 def body(queries, corpus, candidates, threshold):
@@ -14,7 +32,7 @@
     cutoff = threshold.astype(jnp.float32) * 0.01
     owner = lax.axis_index(("rows", "feat"))
     full_rows = lax.all_gather(queries, "feat", axis=1, tiled=True)
-    whole = lax.all_gather(full_rows, "rows", axis=0, tiled=True)
+    whole = laid_out(doubled(full_rows, "rows"), 0)
     query_count = whole.shape[0]
     block = 2048
     corpus_blocks = corpus.reshape(rows_dev // block, block, width)

time: 178 us -> 149 us (0.84)
  blocking collectives: 56.8 us -> 13.1 us
  waiting for transfers between devices: 12.4 us -> 21.8 us
  starting transfers between devices: 14.4 us -> 19.5 us
    all_gather x1 -> x0, blocking collectives: 43.7 us -> none  [body(): whole = lax.all_gather(full_rows, 'rows', axis=0, tiled=True)]
    ppermute x0 -> x4, starting transfers between devices: none -> 6.25 us  [doubled(): other = lax.ppermute(pieces, axis, [(i, i ^ bit) for i in range(peers)])]
    all_to_all x1, waiting for transfers between devices: 0.01 us -> 6.11 us  [body(): lax.all_to_all(partials, 'rows', split_axis=0, concat_axis=0, tiled=True)]
    ppermute x0 -> x4, waiting for transfers between devices: none -> 4.92 us  [doubled(): other = lax.ppermute(pieces, axis, [(i, i ^ bit) for i in range(peers)])]
    reshape x3, local copies, waits for them, and re-layouts: 0.31 us -> 2.46 us  [body(): flat_ids = candidates.reshape(-1)]
    another operation x3 -> x8, other arithmetic: 9.61 us -> 9.79 us
    unnamed x14 -> x12, local copies, waits for them, and re-layouts: 17.2 us -> 17 us
  transfers between devices with their start and end apart: 3 -> 7, of which waited for: 2 -> 4; matrix products, arithmetic and copies ran while one was open for 17% -> 31% of each run, Pallas kernels for 0% -> 0%
where the time goes in v1:
time: 149 us; the launch traced here: 148 us
  local copies, waits for them, and re-layouts  61.3 us (41%)
  waiting for transfers between devices  21.8 us (15%)
  starting transfers between devices  19.5 us (13%)
  matrix products  18.4 us (12%)
  blocking collectives  13.1 us (9%)
  other arithmetic  12.7 us (9%)
    gather x1, local copies, waits for them, and re-layouts, body(): answers.reshape(shards, capacity)[target, rank]  19 us
    dot_general x8, matrix products, visit(): lax.dot_general(whole, block_rows, (((1,), (1,)), ((), ())), preferred_el...  18.4 us
    unnamed x12, local copies, waits for them, and re-layouts  17 us
    another operation x3, other arithmetic  9.61 us
    gather x1, local copies, waits for them, and re-layouts, body(): picked = corpus[received[:, 0]]  8.48 us
    gather x1, local copies, waits for them, and re-layouts, body(): asked = whole[received[:, 1]]  6.72 us
    ppermute x4, starting transfers between devices, doubled(): other = lax.ppermute(pieces, axis, [(i, i ^ bit) for i in range(peers)])  6.25 us
    all_to_all x1, waiting for transfers between devices, body(): lax.all_to_all(partials, 'rows', split_axis=0, concat_axis=0, tiled=True)  6.11 us
  transfers between devices with their start and end apart: 7, of which 4 were waited for; matrix products, arithmetic and copies ran while one was open for 31% of the time, Pallas kernels for 0%

profile of v1, /device:TPU:0, one launch (start us, length us, event | category | flops | bytes accessed | tf_op | source)
XLA Modules:
  0.0 148.1 jit_solution(15506852797543582765)
XLA Ops:
  1.4 2.0 %all_gather.3 = bf16[64,128]{0,1:T(8,128)(2,1)S(1)} all-gather(bf16[64,64]{0,1:T(8,128)(2,1)S(1)} %copy.42), channel_id=1, replica_groups=mesh['rows'=16,'feat'=2] {'feat'}, dimensions={1}, use_global_device_ids=true | all-gather | bytes 24576 | tf_op jit(solution)/shard_map/all_gather | solution.py:34
  3.4 2.9 %collective-permute-start = (bf16[1,64,128]{1,2,0:T(8,128)(2,1)S(1)}, bf16[1,64,128]{1,2,0:T(8,128)(2,1)S(1)}, u32[]{:S(2)}, u32[]{:S(2)}) collective-permute-start(bf16[1,64,128]{1,2,0:T(8,128)(2,1)S(1)} %bitcast.57), channel_id=1, source_target_pairs={{0,2},{2,0},{4,6},{6,4},{8,10},{10,8},{12,14},{14,12},{16,18},{18,... | collective-permute-start | bytes 49160 | tf_op jit(solution)/shard_map/ppermute | solution.py:18
  7.1 0.8 reshape.231
  7.9 0.8 reshape.230
  8.9 9.2 %reduce-window.6 = s32[32,25,128]{2,1,0:T(8,128)S(1)} reduce-window(s32[32,25,128]{2,1,0:T(8,128)S(1)} %fusion.6, s32[]{:T(128)} %constant.23.clone.1), window={size=1x1x128 pad=0_0x0_0x127_0}, to_apply=%region_4.5 | reduce-window | flops 13004800 | bytes 819204 | tf_op jit(solution)/shard_map/reduce-window
  20.6 13.7 %scatter_custom_fusion = s32[3200,2]{1,0:T(8,128)S(1)} fusion(s32[3200]{0:T(1024)S(1)} %broadcast_select_fusion, s32[3200,2]{1,0:T(8,128)S(1)} %copy.47, s32[]{:T(128)} %constant.23.clone.1), kind=kCustom, calls=%fused_computation.11 | custom fusion | bytes 25604
  34.3 1.3 reshape.234
  35.6 5.9 %all-to-all-start.2 = ((s32[16,2,200]{2,1,0:T(2,128)}), s32[16,2,200]{2,1,0:T(2,128)S(1)}, u32[]{:S(2)}, u32[]{:S(2)}) async-start(s32[16,2,200]{2,1,0:T(2,128)} %reshape.234), calls=%async_computation.2 | async-start | bytes 65536 | tf_op jit(solution)/shard_map/all_to_all | solution.py:60
  41.7 2.0 %collective-permute-start.1 = (bf16[2,64,128]{1,2,0:T(8,128)(2,1)S(1)}, bf16[2,64,128]{1,2,0:T(8,128)(2,1)S(1)}, u32[]{:S(2)}, u32[]{:S(2)}) collective-permute-start(bf16[2,64,128]{1,2,0:T(8,128)(2,1)S(1)} %get-tuple-element.64), channel_id=1, source_target_pairs={{0,4},{2,6},{4,0},{6,2},{8,12},{10,14},{12,8},{14,10},{16,20},{18,... | collective-permute-start | bytes 98312 | tf_op jit(solution)/shard_map/ppermute | solution.py:18
  43.7 5.3 %all-to-all-done.2 = s32[16,2,200]{2,1,0:T(2,128)S(1)} async-done(((s32[16,2,200]{2,1,0:T(2,128)}), s32[16,2,200]{2,1,0:T(2,128)S(1)}, u32[]{:S(2)}, u32[]{:S(2)}) %all-to-all-start.2) | async-done | bytes 25632 | tf_op jit(solution)/shard_map/all_to_all | solution.py:60
  49.0 3.7 %all_to_all.30 = s32[16,2,200]{2,0,1:T(8,128)S(1)} all-to-all(s32[16,2,200]{2,0,1:T(8,128)S(1)} %copy.48), channel_id=1, replica_groups=mesh['rows'=16,'feat'=2] {'feat'}, dimensions={1} | all-to-all | bytes 51200 | tf_op jit(solution)/shard_map/all_to_all | solution.py:59
  53.2 1.7 %fusion.19 = (s32[3200,1]{1,0:T(8,128)}, s32[3200,1]{1,0:T(8,128)S(1)}) fusion(s32[3200,2]{1,0:T(8,128)S(1)} %reshape.235), kind=kLoop, calls=%fused_computation.72 | loop fusion | bytes 51200 | tf_op jit(solution)/shard_map/slice | solution.py:74
  54.9 1.9 %copy.60 = s32[3200,1]{0,1:T(1,128)S(1)} copy(s32[3200,1]{1,0:T(8,128)} %get-tuple-element.61) | data formatting | bytes 25600
  58.2 4.9 %collective-permute-done.2 = bf16[4,64,128]{1,2,0:T(8,128)(2,1)S(1)} collective-permute-done((bf16[4,64,128]{1,2,0:T(8,128)(2,1)S(1)}, bf16[4,64,128]{1,2,0:T(8,128)(2,1)S(1)}, u32[]{:S(2)}, u32[]{:S(2)}) %collective-permute-start.2) | collective-permute-done | bytes 65568 | tf_op jit(solution)/shard_map/ppermute | solution.py:18
  64.1 8.5 %gather_fusion = bf16[3200,128]{1,0:T(8,128)(2,1)S(1)} fusion(bf16[16384,128]{1,0:T(8,128)(2,1)} %param.7, s32[4096]{0:T(1024)S(1)} %pad_clamp_fusion.1), kind=kCustom, calls=%fused_computation | custom fusion | bytes 1651200 | tf_op jit(solution)/shard_map/gather | solution.py:73
  72.7 6.7 %gather_fusion.1 = bf16[3200,128]{1,0:T(8,128)(2,1)S(1)} fusion(bf16[1024,128]{1,0:T(8,128)(2,1)S(1)} %bitcast.49, s32[4096]{0:T(1024)S(1)} %pad_clamp_fusion), kind=kCustom, calls=%fused_computation.1 | custom fusion | bytes 1651200 | tf_op jit(solution)/shard_map/gather | solution.py:74
  79.5 18.8 %while.11 = (s32[]{:T(128)}, f32[1024]{0:T(1024)S(1)}, bf16[8,2048,128]{2,1,0:T(8,128)(2,1)}, bf16[1024,128]{1,0:T(8,128)(2,1)S(1)}, f32[1024]{0:T(1024)S(1)}, /*index=5*/s32[]{:T(128)}, s32[]{:T(128)}) while((s32[]{:T(128)}, f32[1024]{0:T(1024)S(1)}, bf16[8,2048,128]{2,1,0:T(8,128)(2,1)}, bf16[1024,128]{1,0:T(8,128)(2,1)S(1)}, ...), condition=%wide.region_2.3_spmd.clone, body=%wide.region_0.2_spmd.clone.sunk | while | flops 543163392 | bytes 807511 | solution.py:46
  79.5 2.3 %maximum_reduce_fusion.2 = f32[1024]{0:T(1024)S(1)} fusion(bf16[1024,128]{1,0:T(8,128)(2,1)S(1)} %get-tuple-element.117, f32[1024]{0:T(1024)S(1)} %get-tuple-element.118, bf16[8,2048,128]{2,1,0:T(8,128)(2,1)} %get-tuple-element.116, s32[]{:T(128)} %get-tuple-element.107), kind=kOutput, calls=%fused_computation.4.clone.1 | convolution fusion | flops 543161344 | bytes 795136 | tf_op jit(solution)/shard_map/while/body/eval_jaxpr/dot_general | solution.py:41
  81.8 2.3 %maximum_reduce_fusion.2 = f32[1024]{0:T(1024)S(1)} fusion(bf16[1024,128]{1,0:T(8,128)(2,1)S(1)} %get-tuple-element.117, f32[1024]{0:T(1024)S(1)} %get-tuple-element.118, bf16[8,2048,128]{2,1,0:T(8,128)(2,1)} %get-tuple-element.116, s32[]{:T(128)} %get-tuple-element.107), kind=kOutput, calls=%fused_computation.4.clone.1 | convolution fusion | flops 543161344 | bytes 795136 | tf_op jit(solution)/shard_map/while/body/eval_jaxpr/dot_general | solution.py:41
  84.2 2.3 %maximum_reduce_fusion.2 = f32[1024]{0:T(1024)S(1)} fusion(bf16[1024,128]{1,0:T(8,128)(2,1)S(1)} %get-tuple-element.117, f32[1024]{0:T(1024)S(1)} %get-tuple-element.118, bf16[8,2048,128]{2,1,0:T(8,128)(2,1)} %get-tuple-element.116, s32[]{:T(128)} %get-tuple-element.107), kind=kOutput, calls=%fused_computation.4.clone.1 | convolution fusion | flops 543161344 | bytes 795136 | tf_op jit(solution)/shard_map/while/body/eval_jaxpr/dot_general | solution.py:41
  86.5 2.3 %maximum_reduce_fusion.2 = f32[1024]{0:T(1024)S(1)} fusion(bf16[1024,128]{1,0:T(8,128)(2,1)S(1)} %get-tuple-element.117, f32[1024]{0:T(1024)S(1)} %get-tuple-element.118, bf16[8,2048,128]{2,1,0:T(8,128)(2,1)} %get-tuple-element.116, s32[]{:T(128)} %get-tuple-element.107), kind=kOutput, calls=%fused_computation.4.clone.1 | convolution fusion | flops 543161344 | bytes 795136 | tf_op jit(solution)/shard_map/while/body/eval_jaxpr/dot_general | solution.py:41
  88.9 2.3 %maximum_reduce_fusion.2 = f32[1024]{0:T(1024)S(1)} fusion(bf16[1024,128]{1,0:T(8,128)(2,1)S(1)} %get-tuple-element.117, f32[1024]{0:T(1024)S(1)} %get-tuple-element.118, bf16[8,2048,128]{2,1,0:T(8,128)(2,1)} %get-tuple-element.116, s32[]{:T(128)} %get-tuple-element.107), kind=kOutput, calls=%fused_computation.4.clone.1 | convolution fusion | flops 543161344 | bytes 795136 | tf_op jit(solution)/shard_map/while/body/eval_jaxpr/dot_general | solution.py:41
  91.2 2.3 %maximum_reduce_fusion.2 = f32[1024]{0:T(1024)S(1)} fusion(bf16[1024,128]{1,0:T(8,128)(2,1)S(1)} %get-tuple-element.117, f32[1024]{0:T(1024)S(1)} %get-tuple-element.118, bf16[8,2048,128]{2,1,0:T(8,128)(2,1)} %get-tuple-element.116, s32[]{:T(128)} %get-tuple-element.107), kind=kOutput, calls=%fused_computation.4.clone.1 | convolution fusion | flops 543161344 | bytes 795136 | tf_op jit(solution)/shard_map/while/body/eval_jaxpr/dot_general | solution.py:41
  93.6 2.3 %maximum_reduce_fusion.2 = f32[1024]{0:T(1024)S(1)} fusion(bf16[1024,128]{1,0:T(8,128)(2,1)S(1)} %get-tuple-element.117, f32[1024]{0:T(1024)S(1)} %get-tuple-element.118, bf16[8,2048,128]{2,1,0:T(8,128)(2,1)} %get-tuple-element.116, s32[]{:T(128)} %get-tuple-element.107), kind=kOutput, calls=%fused_computation.4.clone.1 | convolution fusion | flops 543161344 | bytes 795136 | tf_op jit(solution)/shard_map/while/body/eval_jaxpr/dot_general | solution.py:41
  95.9 2.3 %maximum_reduce_fusion.2 = f32[1024]{0:T(1024)S(1)} fusion(bf16[1024,128]{1,0:T(8,128)(2,1)S(1)} %get-tuple-element.117, f32[1024]{0:T(1024)S(1)} %get-tuple-element.118, bf16[8,2048,128]{2,1,0:T(8,128)(2,1)} %get-tuple-element.116, s32[]{:T(128)} %get-tuple-element.107), kind=kOutput, calls=%fused_computation.4.clone.1 | convolution fusion | flops 543161344 | bytes 795136 | tf_op jit(solution)/shard_map/while/body/eval_jaxpr/dot_general | solution.py:41
  98.9 3.8 %all-to-all-start = ((f32[16,2,32]{2,1,0:T(2,128)}), f32[16,2,32]{2,1,0:T(2,128)S(1)}, u32[]{:S(2)}, u32[]{:S(2)}) async-start(f32[16,2,32]{2,1,0:T(2,128)} %reshape.229), calls=%async_computation | async-start | bytes 32768 | tf_op jit(solution)/shard_map/all_to_all | solution.py:88
  104.0 6.1 %all-to-all-done = f32[16,2,32]{2,1,0:T(2,128)S(1)} async-done(((f32[16,2,32]{2,1,0:T(2,128)}), f32[16,2,32]{2,1,0:T(2,128)S(1)}, u32[]{:S(2)}, u32[]{:S(2)}) %all-to-all-start) | async-done | bytes 4128 | tf_op jit(solution)/shard_map/all_to_all | solution.py:88
  110.2 3.7 %all_to_all.31 = f32[2,1,512]{2,1,0:T(1,128)S(1)} all-to-all(f32[2,1,512]{2,1,0:T(1,128)S(1)} %reshape.281), channel_id=1, replica_groups=mesh['rows'=16,'feat'=2] {'feat'}, dimensions={0} | all-to-all | bytes 8192 | tf_op jit(solution)/shard_map/all_to_all | solution.py:87
  113.8 3.5 %all-to-all-start.4 = ((f32[16,2,100]{2,1,0:T(2,128)}), f32[16,2,100]{2,1,0:T(2,128)S(1)}, u32[]{:S(2)}, u32[]{:S(2)}) async-start(f32[16,2,100]{2,1,0:T(2,128)} %reshape.236), calls=%async_computation.4 | async-start | bytes 32768 | tf_op jit(solution)/shard_map/all_to_all | solution.py:81
  119.1 5.5 %all-to-all-done.4 = f32[16,2,100]{2,1,0:T(2,128)S(1)} async-done(((f32[16,2,100]{2,1,0:T(2,128)}), f32[16,2,100]{2,1,0:T(2,128)S(1)}, u32[]{:S(2)}, u32[]{:S(2)}) %all-to-all-start.4) | async-done | bytes 12832 | tf_op jit(solution)/shard_map/all_to_all | solution.py:81
  124.7 3.7 %all_to_all.32 = f32[16,2,100]{2,0,1:T(8,128)S(1)} all-to-all(f32[16,2,100]{2,0,1:T(8,128)S(1)} %copy.52), channel_id=1, replica_groups=mesh['rows'=16,'feat'=2] {'feat'}, dimensions={1} | all-to-all | bytes 25600 | tf_op jit(solution)/shard_map/all_to_all | solution.py:80
  128.4 19.0 %gather_fusion.2 = f32[3200]{0:T(1024)S(1)} fusion(f32[32,100]{1,0:T(8,128)S(1)} %bitcast.48, s32[3200]{0:T(1024)S(1)} %get-tuple-element.58), kind=kCustom, calls=%fused_computation.2 | custom fusion | bytes 51200 | tf_op jit(solution)/shard_map/gather | solution.py:96
  (67 shorter events, 11.7 us)
Async XLA Ops:
  3.4 38.2 %collective-permute-start = (bf16[1,64,128]{1,2,0:T(8,128)(2,1)S(1)}, bf16[1,64,128]{1,2,0:T(8,128)(2,1)S(1)}, u32[]{:S(2)}, u32[]{:S(2)}) collective-permute-start(bf16[1,64,128]{1,2,0:T(8,128)(2,1)S(1)} %bitcast.57), channel_id=1, source_target_pairs={{0,2},{2,0},{4,6},{6,4},{8,10},{10,8},{12,14},{14,12},{16,18},{18,... | collective-permute-start | bytes 49160 | tf_op jit(solution)/shard_map/ppermute | solution.py:18
  8.8 11.0 %copy-start.2 = (s32[2]{0:T(128)S(1)}, s32[2]{0:T(128)}, u32[]{:S(2)}) copy-start(s32[2]{0:T(128)} %constant.70) | copy-start | bytes 28
  8.8 11.1 %copy-start.1 = (s32[2]{0:T(128)S(1)}, s32[2]{0:T(128)}, u32[]{:S(2)}) copy-start(s32[2]{0:T(128)} %constant.67) | copy-start | bytes 28
  20.6 20.9 %copy-start = (s32[1024]{0:T(1024)S(1)}, s32[1024]{0:T(1024)}, u32[]{:S(2)}) copy-start(s32[1024]{0:T(1024)} %param.9) | copy-start | bytes 12292
  35.6 13.3 %all-to-all-start.2 = ((s32[16,2,200]{2,1,0:T(2,128)}), s32[16,2,200]{2,1,0:T(2,128)S(1)}, u32[]{:S(2)}, u32[]{:S(2)}) async-start(s32[16,2,200]{2,1,0:T(2,128)} %reshape.234), calls=%async_computation.2 | async-start | bytes 65536 | tf_op jit(solution)/shard_map/all_to_all | solution.py:60
  41.7 15.7 %collective-permute-start.1 = (bf16[2,64,128]{1,2,0:T(8,128)(2,1)S(1)}, bf16[2,64,128]{1,2,0:T(8,128)(2,1)S(1)}, u32[]{:S(2)}, u32[]{:S(2)}) collective-permute-start(bf16[2,64,128]{1,2,0:T(8,128)(2,1)S(1)} %get-tuple-element.64), channel_id=1, source_target_pairs={{0,4},{2,6},{4,0},{6,2},{8,12},{10,14},{12,8},{14,10},{16,20},{18,... | collective-permute-start | bytes 98312 | tf_op jit(solution)/shard_map/ppermute | solution.py:18
  57.5 5.6 %collective-permute-start.2 = (bf16[4,64,128]{1,2,0:T(8,128)(2,1)S(1)}, bf16[4,64,128]{1,2,0:T(8,128)(2,1)S(1)}, u32[]{:S(2)}, u32[]{:S(2)}) collective-permute-start(bf16[4,64,128]{1,2,0:T(8,128)(2,1)S(1)} %bitcast.55), channel_id=1, source_target_pairs={{0,8},{2,10},{4,12},{6,14},{8,0},{10,2},{12,4},{14,6},{16,24},{18,... | collective-permute-start | bytes 196616 | tf_op jit(solution)/shard_map/ppermute | solution.py:18
  63.4 9.2 %collective-permute-start.3 = (bf16[8,64,128]{2,1,0:T(8,128)(2,1)S(1)}, bf16[8,64,128]{2,1,0:T(8,128)(2,1)S(1)}, u32[]{:S(2)}, u32[]{:S(2)}) collective-permute-start(bf16[8,64,128]{2,1,0:T(8,128)(2,1)S(1)} %bitcast.53), channel_id=1, source_target_pairs={{0,16},{2,18},{4,20},{6,22},{8,24},{10,26},{12,28},{14,30},{16,0},... | collective-permute-start | bytes 393224 | tf_op jit(solution)/shard_map/ppermute | solution.py:18
  98.9 11.1 %all-to-all-start = ((f32[16,2,32]{2,1,0:T(2,128)}), f32[16,2,32]{2,1,0:T(2,128)S(1)}, u32[]{:S(2)}, u32[]{:S(2)}) async-start(f32[16,2,32]{2,1,0:T(2,128)} %reshape.229), calls=%async_computation | async-start | bytes 32768 | tf_op jit(solution)/shard_map/all_to_all | solution.py:88
  113.8 10.8 %all-to-all-start.4 = ((f32[16,2,100]{2,1,0:T(2,128)}), f32[16,2,100]{2,1,0:T(2,128)S(1)}, u32[]{:S(2)}, u32[]{:S(2)}) async-start(f32[16,2,100]{2,1,0:T(2,128)} %reshape.236), calls=%async_computation.4 | async-start | bytes 32768 | tf_op jit(solution)/shard_map/all_to_all | solution.py:81
